TPU v7x, 256 devices: a whole 4x4x8 slice. The times are simulated.
256 devices in a mesh: chain: 64 (over z, x, core), col: 4 (over y).
Axes of the slice: x: 4, y: 4, z: 8, core: 2. Of those that a mesh axis runs over, the one named last changes fastest.
Arguments:
- inverses: float32 [64, 2, 512, 512], P('chain', None, None, 'col'), may hold values from -3 to 3
- couplings: float32 [64, 2, 512, 512], P('chain', None, None, 'col'), may hold values from -3 to 3
- sources: float32 [64, 2, 512, 1024], P('chain', None, None, 'col'), may hold values from -6 to 6
- counts: int32 [64], P('chain'), may hold values from 384 to 512, as said below
Outputs:
- fields: float32 [64, 2, 512, 1024], P('chain', None, None, 'col')
Inputs may be any that keep to these rules, and one draw needn't show every extreme that they name: `counts`: some slice has exactly 512 orbitals in use.
All inputs are finite; a program needn't handle non-finite values.
Results may differ from a plain program's by a relative error of at most 0.0003.
Values sent between devices are 32-bit elements; how exact they have to be, the bound alone decides.
A program may use at most 128 MiB of HBM per device.

v0:
```python
import functools

import jax
import jax.numpy as jnp
from jax import lax
from jax.experimental import pallas as pl
from jax.experimental.pallas import tpu as pltpu
from jax.sharding import PartitionSpec as P

MESH = pl.DeviceIdType.MESH
PLANE = 8
ROWS = 4


def split(value):
    high = value.astype(jnp.bfloat16)
    return high, (value - high.astype(jnp.float32)).astype(jnp.bfloat16)


def product(real, imag, high_ref, low_ref):
    count, width = real.shape
    tile = min(256, width)
    real_high, real_low = split(real)
    imag_high, imag_low = split(imag)
    high = jnp.concatenate([real_high, imag_high], axis=0)
    both = jnp.concatenate([real_high, imag_high, real_low, imag_low], axis=0)

    def against(columns):
        wide = jnp.dot(both, high_ref[:, columns], preferred_element_type=jnp.float32)
        narrow = jnp.dot(high, low_ref[:, columns], preferred_element_type=jnp.float32)
        return wide[: 2 * count] + (wide[2 * count :] + narrow)

    reals, imags = [], []
    for start in range(0, width, tile):
        by_real = against(slice(start, start + tile))
        by_imag = against(slice(width + start, width + start + tile))
        reals.append(by_real[:count] - by_imag[count:])
        imags.append(by_imag[:count] + by_real[count:])
    return jnp.concatenate(reals, axis=1), jnp.concatenate(imags, axis=1)


def kernel(
    planes,
    inverse_ref,
    coupling_ref,
    source_ref,
    active_ref,
    out_ref,
    inv,
    cpl,
    src,
    inv_high,
    inv_low,
    own_high,
    own_low,
    pair_high,
    pair_low,
    even_map,
    even_in,
    even_offset,
    offset,
    map_in,
    map_out,
    off_in,
    off_out,
    whole,
    whole_high,
    whole_low,
    z_in,
    x_in,
    state,
    local_sem,
    gather_send,
    gather_recv,
    core_send,
    core_recv,
    map_send,
    map_recv,
    off_send,
    off_recv,
    z_recv,
    x_recv,
    out_send,
    pass_send,
):
    width = inv_high.shape[0]
    block = width // ROWS
    columns = offset.shape[0]
    map_step = block // map_recv.shape[0]
    off_step = columns // off_recv.shape[0]
    end_step = columns // z_recv.shape[0]

    place = lax.axis_index("chain")
    col = lax.axis_index("col")
    z = place // PLANE
    x = (place % PLANE) // 2
    core = place % 2
    up, down, across = (col + 1) % ROWS, (col + 3) % ROWS, (col + 2) % ROWS

    def at(z_to, x_to, core_to):
        return {"chain": z_to * PLANE + x_to * 2 + core_to, "col": col}

    partner = at(z, x, 1 - core)
    upward = {"chain": place, "col": up}
    downward = {"chain": place, "col": down}
    x_next, x_before = (x + 1) % 4, (x + 3) % 4
    z_next, z_before = (z + 1) % planes, (z + planes - 1) % planes

    barrier = pltpu.get_barrier_semaphore()
    greeted = (
        upward,
        downward,
        partner,
        at(z, x_next, core),
        at(z, x_before, core),
        at(z, x_next, 1 - core),
        at(z, x_before, 1 - core),
        at(z_next, x, core),
        at(z_before, x, core),
    )
    for device in greeted:
        pl.semaphore_signal(barrier, inc=1, device_id=device, device_id_type=MESH)
    pl.semaphore_wait(barrier, len(greeted))

    def remote(source, target, send, recv, device):
        return pltpu.make_async_remote_copy(
            src_ref=source,
            dst_ref=target,
            send_sem=send,
            recv_sem=recv,
            device_id=device,
            device_id_type=MESH,
        )

    def ring(own, held, which):
        send, recv = gather_send.at[which], gather_recv.at[which]
        first, second = held.at[:, 0], held.at[:, 1]
        own_first, own_second = own
        return [
            remote(own_first, first.at[col], send.at[0], recv.at[0], upward),
            remote(own_second, second.at[col], send.at[1], recv.at[1], downward),
            remote(own_second, second.at[col], send.at[2], recv.at[2], upward),
            remote(own_first, first.at[col], send.at[3], recv.at[3], downward),
            remote(first.at[down], first.at[down], send.at[4], recv.at[4], upward),
            remote(second.at[up], second.at[up], send.at[5], recv.at[5], downward),
        ]

    inv_ring = ring((inverse_ref.at[0, 0], inverse_ref.at[0, 1]), inv, 0)
    cpl_ring = ring((coupling_ref.at[0, 0], coupling_ref.at[0, 1]), cpl, 1)
    for copy in inv_ring[:4]:
        copy.start()
    own_inv = pltpu.make_async_copy(inverse_ref.at[0], inv.at[col], local_sem.at[0])
    own_cpl = pltpu.make_async_copy(coupling_ref.at[0], cpl.at[col], local_sem.at[1])
    own_src = pltpu.make_async_copy(source_ref.at[0], src, local_sem.at[2])
    own_inv.start()
    own_cpl.start()
    own_src.start()

    active = active_ref[0:1, :]

    def take_inverse(which):
        rows = pl.ds(pl.multiple_of(which * block, block), block)
        for part in range(2):
            high, low = split(inv[which, part].T * active)
            inv_high[rows, part * width : (part + 1) * width] = high
            inv_low[rows, part * width : (part + 1) * width] = low

    own_inv.wait()
    take_inverse(col)
    inv_ring[0].wait_recv()
    inv_ring[4].start()
    inv_ring[1].wait_recv()
    inv_ring[5].start()
    for copy in cpl_ring[:4]:
        copy.start()
    inv_ring[2].wait_recv()
    take_inverse(down)
    inv_ring[3].wait_recv()
    take_inverse(up)
    inv_ring[4].wait_recv()
    inv_ring[5].wait_recv()
    take_inverse(across)

    own_src.wait()
    for start in range(0, columns, block):
        real, imag = product(
            src[0, :, start : start + block].T, src[1, :, start : start + block].T, inv_high, inv_low
        )
        offset[start : start + block, :width] = real
        offset[start : start + block, width:] = imag

    even_offset_copy = remote(offset, even_offset, core_send.at[ROWS], core_recv.at[ROWS], partner)

    @pl.when(core == 0)
    def _():
        even_offset_copy.start()

    def even_map_copy(which):
        return remote(
            even_map.at[which], even_in.at[which], core_send.at[which], core_recv.at[which], partner
        )

    def take_coupling(which):
        rows = pl.ds(pl.multiple_of(which * block, block), block)
        real, imag = product(cpl[which, 0].T, cpl[which, 1].T, inv_high, inv_low)
        for part, value in enumerate((real, imag)):
            high, low = split(value)
            own_high[rows, part * width : (part + 1) * width] = high
            own_low[rows, part * width : (part + 1) * width] = low

        @pl.when(core == 0)
        def _():
            even_map[which, :, :width] = real
            even_map[which, :, width:] = imag
            even_map_copy(which).start()

    own_cpl.wait()
    take_coupling(col)
    cpl_ring[0].wait_recv()
    cpl_ring[4].start()
    cpl_ring[1].wait_recv()
    cpl_ring[5].start()
    cpl_ring[2].wait_recv()
    take_coupling(down)
    cpl_ring[3].wait_recv()
    take_coupling(up)
    cpl_ring[4].wait_recv()
    cpl_ring[5].wait_recv()
    take_coupling(across)
    for copy in inv_ring + cpl_ring:
        copy.wait_send()

    def rows_of(step, index):
        return pl.ds(pl.multiple_of(index * step, step), step)

    def chunk(ref, rows):
        return ref[rows, :width], ref[rows, width:]

    def put(ref, rows, value):
        ref[rows, :width] = value[0]
        ref[rows, width:] = value[1]

    def plus(value, other):
        return value[0] + other[0], value[1] + other[1]

    next_odd = at(z, x_next, 1)

    def map_copy(index):
        rows = rows_of(map_step, index)
        return remote(
            map_out.at[rows], map_in.at[rows], map_send.at[index], map_recv.at[index], next_odd
        )

    def off_copy(index):
        rows = rows_of(off_step, index)
        return remote(
            off_out.at[rows], off_in.at[rows], off_send.at[index], off_recv.at[index], next_odd
        )

    whole_ring = ring((map_out.at[:, :width], map_out.at[:, width:]), whole, 2)

    @pl.when(core == 1)
    def _():
        def compose(which):
            rows = pl.ds(pl.multiple_of(which * block, block), block)
            even_map_copy(which).wait_recv()
            value = product(even_in[which, :, :width], even_in[which, :, width:], own_high, own_low)
            for part in range(2):
                high, low = split(value[part])
                pair_high[rows, part * width : (part + 1) * width] = high
                pair_low[rows, part * width : (part + 1) * width] = low
            return value

        first = compose(col)

        @pl.when(x == 0)
        def _():
            put(map_out, slice(None), first)
            for index in range(map_recv.shape[0]):
                map_copy(index).start()

        for which in (down, up, across):
            compose(which)
        even_offset_copy.wait_recv()

        def compose_offset(index, carry):
            rows = rows_of(block, index)
            value = product(*chunk(even_offset, rows), own_high, own_low)
            put(offset, rows, plus(value, chunk(offset, rows)))
            return carry

        lax.fori_loop(0, columns // block, compose_offset, 0)

        @pl.when(x == 0)
        def _():
            off_out[...] = offset[...]
            for index in range(off_recv.shape[0]):
                off_copy(index).start()

        @pl.when(x > 0)
        def _():
            def map_sweep(index, carry):
                rows = rows_of(map_step, index)
                map_copy(index).wait_recv()
                put(map_out, rows, product(*chunk(map_in, rows), pair_high, pair_low))

                @pl.when(x < 3)
                def _():
                    map_copy(index).start()

                return carry

            lax.fori_loop(0, map_recv.shape[0], map_sweep, 0)

            def off_sweep(index, carry):
                rows = rows_of(off_step, index)
                off_copy(index).wait_recv()
                value = product(*chunk(off_in, rows), pair_high, pair_low)
                put(off_out, rows, plus(value, chunk(offset, rows)))

                @pl.when(x < 3)
                def _():
                    off_copy(index).start()

                return carry

            @pl.when(x == 3)
            def _():
                for copy in whole_ring[:4]:
                    copy.start()

            lax.fori_loop(0, off_recv.shape[0] // 2, off_sweep, 0)

            @pl.when(x == 3)
            def _():
                whole_ring[0].wait_recv()
                whole_ring[4].start()
                whole_ring[1].wait_recv()
                whole_ring[5].start()

            lax.fori_loop(off_recv.shape[0] // 2, off_recv.shape[0], off_sweep, 0)

        @pl.when(x < 3)
        def _():
            for index in range(map_recv.shape[0]):
                map_copy(index).wait_send()
            for index in range(off_recv.shape[0]):
                off_copy(index).wait_send()

    ends = z_recv.shape[0]

    def z_copy(index):
        rows = rows_of(end_step, index)
        return remote(
            state.at[rows], z_in.at[rows], out_send.at[index], z_recv.at[index], at(z_next, 3, 1)
        )

    def enter_copy(index):
        rows = rows_of(end_step, index)
        return remote(
            z_in.at[rows], x_in.at[rows], pass_send.at[index], x_recv.at[index], at(z, 0, 1)
        )

    def x_copy(index):
        rows = rows_of(end_step, index)
        device = at(z, x_next, jnp.where(x_next == 3, 0, 1))
        return remote(state.at[rows], x_in.at[rows], out_send.at[index], x_recv.at[index], device)

    def pass_copy(index):
        rows = rows_of(end_step, index)
        return remote(
            x_in.at[rows], x_in.at[rows], pass_send.at[index], x_recv.at[index], partner
        )

    @pl.when((core == 1) & (x == 3))
    def _():
        @pl.when(z == 0)
        def _():
            z_in[...] = jnp.zeros_like(z_in)
            state[...] = off_out[...]
            for index in range(ends):
                z_copy(index).start()
            for index in range(ends):
                enter_copy(index).start()

        def take_whole(which):
            rows = pl.ds(pl.multiple_of(which * block, block), block)
            for part in range(2):
                high, low = split(whole[which, part])
                whole_high[rows, part * width : (part + 1) * width] = high
                whole_low[rows, part * width : (part + 1) * width] = low

        for part in range(2):
            whole[col, part] = map_out[:, part * width : (part + 1) * width]
        take_whole(col)
        whole_ring[2].wait_recv()
        take_whole(down)
        whole_ring[3].wait_recv()
        take_whole(up)
        whole_ring[4].wait_recv()
        whole_ring[5].wait_recv()
        take_whole(across)
        for copy in whole_ring:
            copy.wait_send()

        @pl.when(z > 0)
        def _():
            def z_sweep(index, carry):
                rows = rows_of(end_step, index)
                z_copy(index).wait_recv()
                enter_copy(index).start()
                value = product(*chunk(z_in, rows), whole_high, whole_low)
                put(state, rows, plus(value, chunk(off_out, rows)))

                @pl.when(z < planes - 1)
                def _():
                    z_copy(index).start()

                return carry

            lax.fori_loop(0, ends, z_sweep, 0)

        @pl.when(z < planes - 1)
        def _():
            for index in range(ends):
                z_copy(index).wait_send()

        for index in range(ends):
            enter_copy(index).wait_send()

    @pl.when((core == 1) & (x < 3))
    def _():
        def x_sweep(index, carry):
            rows = rows_of(end_step, index)
            x_copy(index).wait_recv()
            pass_copy(index).start()
            value = product(*chunk(x_in, rows), pair_high, pair_low)
            put(state, rows, plus(value, chunk(offset, rows)))
            x_copy(index).start()
            return carry

        lax.fori_loop(0, ends, x_sweep, 0)
        for index in range(ends):
            x_copy(index).wait_send()
            pass_copy(index).wait_send()

    @pl.when(core == 0)
    def _():
        def even_sweep(index, carry):
            rows = rows_of(end_step, index)
            x_copy(index).wait_recv()
            value = product(*chunk(x_in, rows), own_high, own_low)
            put(state, rows, plus(value, chunk(offset, rows)))
            return carry

        lax.fori_loop(0, ends, even_sweep, 0)
        for which in range(ROWS):
            even_map_copy(which).wait_send()
        even_offset_copy.wait_send()

    for start in range(0, columns, block):
        for part in range(2):
            out_ref[0, part, :, start : start + block] = state[
                start : start + block, part * width : (part + 1) * width
            ].T


def local(planes, inverses, couplings, sources, counts):
    width, block = inverses.shape[2], inverses.shape[3]
    columns = sources.shape[3]
    active = (lax.iota(jnp.int32, width) < counts[0]).astype(jnp.float32)
    active = jnp.broadcast_to(active[None], (8, width))
    map_chunks, off_chunks, end_chunks = 4, 8, 8
    single, half = jnp.float32, jnp.bfloat16
    vmem, dma = pltpu.VMEM, pltpu.SemaphoreType.DMA
    held_map = vmem((width, 2 * width), half)
    rows_buffer = vmem((columns, 2 * width), single)
    map_buffer = vmem((block, 2 * width), single)
    any_space = pl.BlockSpec(memory_space=pl.ANY)
    in_vmem = pl.BlockSpec(memory_space=pltpu.VMEM)
    return pl.pallas_call(
        functools.partial(kernel, planes),
        out_shape=jax.ShapeDtypeStruct(sources.shape, single),
        in_specs=[any_space, any_space, any_space, in_vmem],
        out_specs=in_vmem,
        scratch_shapes=[
            vmem((ROWS, 2, width, block), single),
            vmem((ROWS, 2, width, block), single),
            vmem((2, width, columns), single),
            held_map,
            held_map,
            held_map,
            held_map,
            held_map,
            held_map,
            vmem((ROWS, block, 2 * width), single),
            vmem((ROWS, block, 2 * width), single),
            rows_buffer,
            rows_buffer,
            map_buffer,
            map_buffer,
            rows_buffer,
            rows_buffer,
            vmem((ROWS, 2, block, width), single),
            held_map,
            held_map,
            rows_buffer,
            rows_buffer,
            rows_buffer,
            dma((3,)),
            dma((3, 6)),
            dma((3, 6)),
            dma((ROWS + 1,)),
            dma((ROWS + 1,)),
            dma((map_chunks,)),
            dma((map_chunks,)),
            dma((off_chunks,)),
            dma((off_chunks,)),
            dma((end_chunks,)),
            dma((end_chunks,)),
            dma((end_chunks,)),
            dma((end_chunks,)),
        ],
        compiler_params=pltpu.CompilerParams(
            collective_id=0, has_side_effects=True, vmem_limit_bytes=60 * 2**20
        ),
    )(inverses, couplings, sources, active)


def solution(mesh):
    placed = (
        P("chain", None, None, "col"),
        P("chain", None, None, "col"),
        P("chain", None, None, "col"),
        P("chain"),
    )
    return jax.shard_map(
        functools.partial(local, mesh.shape["chain"] // PLANE),
        mesh=mesh,
        in_specs=placed,
        out_specs=P("chain", None, None, "col"),
        check_vma=False,
    )
```

profile of v0, /device:TPU:230, one launch (start us, length us, event | category | flops | bytes accessed | tf_op | source)
XLA Modules:
  0.0 123.9 jit_solution(12574943150094945612)
XLA Ops:
  0.7 0.6 broadcast_in_dim.2.active_ref
  1.3 120.4 %shard_map.46 = f32[1,2,512,256]{3,2,1,0:T(8,128)} custom-call(f32[1,2,512,128]{3,2,1,0:T(8,128)} %inverse_ref.1, f32[1,2,512,128]{3,2,1,0:T(8,128)} %coupling_ref.1, f32[1,2,512,256]{3,2,1,0:T(8,128)} %source_ref.1, f32[8,512]{1,0:T(8,128)} %broadcast_in_dim.2.active_ref), custom_call_target="tpu_custom_call" | custom-call | tf_op jit(solution)/shard_map/pallas_call | solution.py:481
  121.6 2.3 %copy.7 = f32[1,2,512,256]{3,2,1,0:T(8,128)} copy(f32[1,2,512,256]{3,2,1,0:T(8,128)} %shard_map.46) | data formatting | bytes 2097152
  (1 shorter events, 0.0 us)
where the time goes:
time: 124 us
  Pallas kernels  120 us (97%)
  local copies, waits for them, and re-layouts  2.87 us (2%)
    pallas_call x1, Pallas kernels, local(): pl.pallas_call(functools.partial(kernel, planes), out_shape=jax.ShapeDtyp...  120 us

commit v1 on v0

--- a/solution.py
+++ b/solution.py
@@ -44,7 +44,7 @@
     inverse_ref,
     coupling_ref,
     source_ref,
-    active_ref,
+    count_ref,
     out_ref,
     inv,
     cpl,
@@ -82,6 +82,10 @@
     x_recv,
     out_send,
     pass_send,
+    back_send,
+    whole_send,
+    whole_recv,
+    turn_sem,
 ):
     width = inv_high.shape[0]
     block = width // ROWS
@@ -104,23 +108,27 @@
     upward = {"chain": place, "col": up}
     downward = {"chain": place, "col": down}
     x_next, x_before = (x + 1) % 4, (x + 3) % 4
-    z_next, z_before = (z + 1) % planes, (z + planes - 1) % planes
+    odd, last = core == 1, (core == 1) & (x == 3)
 
     barrier = pltpu.get_barrier_semaphore()
-    greeted = (
-        upward,
-        downward,
-        partner,
-        at(z, x_next, core),
-        at(z, x_before, core),
-        at(z, x_next, 1 - core),
-        at(z, x_before, 1 - core),
-        at(z_next, x, core),
-        at(z_before, x, core),
-    )
-    for device in greeted:
+
+    def greet(when, device):
+        @pl.when(when)
+        def _():
+            pl.semaphore_signal(barrier, inc=1, device_id=device, device_id_type=MESH)
+
+        return jnp.where(when, 1, 0)
+
+    for device in (upward, downward, partner):
         pl.semaphore_signal(barrier, inc=1, device_id=device, device_id_type=MESH)
-    pl.semaphore_wait(barrier, len(greeted))
+    greeted = 3
+    greeted += greet(odd, at(z, x_next, 1))
+    greeted += greet(odd, at(z, x_before, 1))
+    greeted += greet(odd & (x < 3), at(z, x_next, 0))
+    greeted += greet((core == 0) & (x > 0), at(z, x_before, 1))
+    greeted += greet(last & (z < planes - 1), at(z + 1, 3, 1))
+    greeted += greet(last & (z > 0), at(z - 1, 3, 1))
+    pl.semaphore_wait(barrier, greeted)
 
     def remote(source, target, send, recv, device):
         return pltpu.make_async_remote_copy(
@@ -147,8 +155,6 @@
 
     inv_ring = ring((inverse_ref.at[0, 0], inverse_ref.at[0, 1]), inv, 0)
     cpl_ring = ring((coupling_ref.at[0, 0], coupling_ref.at[0, 1]), cpl, 1)
-    for copy in inv_ring[:4]:
-        copy.start()
     own_inv = pltpu.make_async_copy(inverse_ref.at[0], inv.at[col], local_sem.at[0])
     own_cpl = pltpu.make_async_copy(coupling_ref.at[0], cpl.at[col], local_sem.at[1])
     own_src = pltpu.make_async_copy(source_ref.at[0], src, local_sem.at[2])
@@ -156,7 +162,14 @@
     own_cpl.start()
     own_src.start()
 
-    active = active_ref[0:1, :]
+    @pl.when(core == 0)
+    def _():
+        pl.semaphore_wait(turn_sem, 1)
+
+    for copy in inv_ring[:4]:
+        copy.start()
+
+    active = (lax.broadcasted_iota(jnp.int32, (1, width), 1) < count_ref[0]).astype(jnp.float32)
 
     def take_inverse(which):
         rows = pl.ds(pl.multiple_of(which * block, block), block)
@@ -181,20 +194,6 @@
     inv_ring[5].wait_recv()
     take_inverse(across)
 
-    own_src.wait()
-    for start in range(0, columns, block):
-        real, imag = product(
-            src[0, :, start : start + block].T, src[1, :, start : start + block].T, inv_high, inv_low
-        )
-        offset[start : start + block, :width] = real
-        offset[start : start + block, width:] = imag
-
-    even_offset_copy = remote(offset, even_offset, core_send.at[ROWS], core_recv.at[ROWS], partner)
-
-    @pl.when(core == 0)
-    def _():
-        even_offset_copy.start()
-
     def even_map_copy(which):
         return remote(
             even_map.at[which], even_in.at[which], core_send.at[which], core_recv.at[which], partner
@@ -216,13 +215,32 @@
 
     own_cpl.wait()
     take_coupling(col)
+    own_src.wait()
+    for start in range(0, columns, block):
+        real, imag = product(
+            src[0, :, start : start + block].T, src[1, :, start : start + block].T, inv_high, inv_low
+        )
+        offset[start : start + block, :width] = real
+        offset[start : start + block, width:] = imag
+
+    even_offset_copy = remote(offset, even_offset, core_send.at[ROWS], core_recv.at[ROWS], partner)
+
+    @pl.when(core == 0)
+    def _():
+        even_offset_copy.start()
+
     cpl_ring[0].wait_recv()
     cpl_ring[4].start()
     cpl_ring[1].wait_recv()
     cpl_ring[5].start()
     cpl_ring[2].wait_recv()
+    cpl_ring[3].wait_recv()
+
+    @pl.when(core == 1)
+    def _():
+        pl.semaphore_signal(turn_sem, inc=1, device_id=partner, device_id_type=MESH)
+
     take_coupling(down)
-    cpl_ring[3].wait_recv()
     take_coupling(up)
     cpl_ring[4].wait_recv()
     cpl_ring[5].wait_recv()
@@ -257,7 +275,20 @@
             off_out.at[rows], off_in.at[rows], off_send.at[index], off_recv.at[index], next_odd
         )
 
-    whole_ring = ring((map_out.at[:, :width], map_out.at[:, width:]), whole, 2)
+    maps = map_recv.shape[0]
+
+    def whole_copy(kind, index):
+        rows = rows_of(map_step, index)
+        send, recv = whole_send.at[kind, index], whole_recv.at[kind, index]
+        if kind < 2:
+            return remote(map_out.at[rows], whole.at[col, rows], send, recv, (upward, downward)[kind])
+        if index < maps // 2:
+            return remote(whole.at[down, rows], whole.at[down, rows], send, recv, upward)
+        return remote(whole.at[up, rows], whole.at[up, rows], send, recv, downward)
+
+    def forward(index):
+        whole_copy(0 if index < maps // 2 else 1, index).wait_recv()
+        whole_copy(2, index).start()
 
     @pl.when(core == 1)
     def _():
@@ -279,8 +310,6 @@
             for index in range(map_recv.shape[0]):
                 map_copy(index).start()
 
-        for which in (down, up, across):
-            compose(which)
         even_offset_copy.wait_recv()
 
         def compose_offset(index, carry):
@@ -297,6 +326,9 @@
             for index in range(off_recv.shape[0]):
                 off_copy(index).start()
 
+        for which in (down, up, across):
+            compose(which)
+
         @pl.when(x > 0)
         def _():
             def map_sweep(index, carry):
@@ -307,6 +339,11 @@
                 @pl.when(x < 3)
                 def _():
                     map_copy(index).start()
+
+                @pl.when(x == 3)
+                def _():
+                    whole_copy(0, index).start()
+                    whole_copy(1, index).start()
 
                 return carry
 
@@ -324,35 +361,58 @@
 
                 return carry
 
-            @pl.when(x == 3)
-            def _():
-                for copy in whole_ring[:4]:
-                    copy.start()
-
-            lax.fori_loop(0, off_recv.shape[0] // 2, off_sweep, 0)
-
-            @pl.when(x == 3)
-            def _():
-                whole_ring[0].wait_recv()
-                whole_ring[4].start()
-                whole_ring[1].wait_recv()
-                whole_ring[5].start()
-
-            lax.fori_loop(off_recv.shape[0] // 2, off_recv.shape[0], off_sweep, 0)
+            done = 0
+            for index in range(maps):
+                until = max(0, 2 * index - maps // 2)
+                if until > done:
+                    lax.fori_loop(done, until, off_sweep, 0)
+                    done = until
+
+                @pl.when(x == 3)
+                def _():
+                    forward(index)
+
+            lax.fori_loop(done, off_recv.shape[0], off_sweep, 0)
 
         @pl.when(x < 3)
         def _():
+            for index in range(maps):
+                whole_copy(0, index).start()
+                whole_copy(1, index).start()
+            for index in range(maps):
+                forward(index)
             for index in range(map_recv.shape[0]):
                 map_copy(index).wait_send()
             for index in range(off_recv.shape[0]):
                 off_copy(index).wait_send()
 
+        def take_whole(which):
+            rows = pl.ds(pl.multiple_of(which * block, block), block)
+            high, low = split(whole[which])
+            whole_high[rows] = high
+            whole_low[rows] = low
+
+        whole[col] = map_out[...]
+        take_whole(col)
+        for index in range(maps // 2, maps):
+            whole_copy(0, index).wait_recv()
+        take_whole(down)
+        for index in range(maps // 2):
+            whole_copy(1, index).wait_recv()
+        take_whole(up)
+        for index in range(maps):
+            whole_copy(2, index).wait_recv()
+        take_whole(across)
+        for kind in range(3):
+            for index in range(maps):
+                whole_copy(kind, index).wait_send()
+
     ends = z_recv.shape[0]
 
     def z_copy(index):
         rows = rows_of(end_step, index)
         return remote(
-            state.at[rows], z_in.at[rows], out_send.at[index], z_recv.at[index], at(z_next, 3, 1)
+            state.at[rows], z_in.at[rows], out_send.at[index], z_recv.at[index], at((z + 1) % planes, 3, 1)
         )
 
     def enter_copy(index):
@@ -361,15 +421,28 @@
             z_in.at[rows], x_in.at[rows], pass_send.at[index], x_recv.at[index], at(z, 0, 1)
         )
 
+    def enter_back_copy(index):
+        rows = rows_of(end_step, index)
+        return remote(
+            z_in.at[rows], x_in.at[rows], back_send.at[index], x_recv.at[index], at(z, 2, 1)
+        )
+
+    def back_copy(index):
+        rows = rows_of(end_step, index)
+        return remote(
+            x_in.at[rows], x_in.at[rows], back_send.at[index], x_recv.at[index], at(z, x_before, 1)
+        )
+
+    def pass_copy(index):
+        rows = rows_of(end_step, index)
+        return remote(
+            x_in.at[rows], x_in.at[rows], pass_send.at[index], x_recv.at[index], partner
+        )
+
     def x_copy(index):
         rows = rows_of(end_step, index)
-        device = at(z, x_next, jnp.where(x_next == 3, 0, 1))
-        return remote(state.at[rows], x_in.at[rows], out_send.at[index], x_recv.at[index], device)
-
-    def pass_copy(index):
-        rows = rows_of(end_step, index)
-        return remote(
-            x_in.at[rows], x_in.at[rows], pass_send.at[index], x_recv.at[index], partner
+        return remote(
+            state.at[rows], x_in.at[rows], out_send.at[index], x_recv.at[index], at(z, x_next, 0)
         )
 
     @pl.when((core == 1) & (x == 3))
@@ -382,26 +455,7 @@
                 z_copy(index).start()
             for index in range(ends):
                 enter_copy(index).start()
-
-        def take_whole(which):
-            rows = pl.ds(pl.multiple_of(which * block, block), block)
-            for part in range(2):
-                high, low = split(whole[which, part])
-                whole_high[rows, part * width : (part + 1) * width] = high
-                whole_low[rows, part * width : (part + 1) * width] = low
-
-        for part in range(2):
-            whole[col, part] = map_out[:, part * width : (part + 1) * width]
-        take_whole(col)
-        whole_ring[2].wait_recv()
-        take_whole(down)
-        whole_ring[3].wait_recv()
-        take_whole(up)
-        whole_ring[4].wait_recv()
-        whole_ring[5].wait_recv()
-        take_whole(across)
-        for copy in whole_ring:
-            copy.wait_send()
+                enter_back_copy(index).start()
 
         @pl.when(z > 0)
         def _():
@@ -409,6 +463,7 @@
                 rows = rows_of(end_step, index)
                 z_copy(index).wait_recv()
                 enter_copy(index).start()
+                enter_back_copy(index).start()
                 value = product(*chunk(z_in, rows), whole_high, whole_low)
                 put(state, rows, plus(value, chunk(off_out, rows)))
 
@@ -427,22 +482,40 @@
 
         for index in range(ends):
             enter_copy(index).wait_send()
+            enter_back_copy(index).wait_send()
 
     @pl.when((core == 1) & (x < 3))
     def _():
         def x_sweep(index, carry):
             rows = rows_of(end_step, index)
             x_copy(index).wait_recv()
-            pass_copy(index).start()
-            value = product(*chunk(x_in, rows), pair_high, pair_low)
-            put(state, rows, plus(value, chunk(offset, rows)))
+
+            @pl.when(x == 2)
+            def _():
+                back_copy(index).start()
+
+            @pl.when(x == 0)
+            def _():
+                pass_copy(index).start()
+
+            value = product(*chunk(x_in, rows), whole_high, whole_low)
+            put(state, rows, plus(value, chunk(off_out, rows)))
             x_copy(index).start()
             return carry
 
         lax.fori_loop(0, ends, x_sweep, 0)
         for index in range(ends):
             x_copy(index).wait_send()
-            pass_copy(index).wait_send()
+
+        @pl.when(x == 2)
+        def _():
+            for index in range(ends):
+                back_copy(index).wait_send()
+
+        @pl.when(x == 0)
+        def _():
+            for index in range(ends):
+                pass_copy(index).wait_send()
 
     @pl.when(core == 0)
     def _():
@@ -468,9 +541,7 @@
 def local(planes, inverses, couplings, sources, counts):
     width, block = inverses.shape[2], inverses.shape[3]
     columns = sources.shape[3]
-    active = (lax.iota(jnp.int32, width) < counts[0]).astype(jnp.float32)
-    active = jnp.broadcast_to(active[None], (8, width))
-    map_chunks, off_chunks, end_chunks = 4, 8, 8
+    map_chunks, off_chunks, end_chunks = 4, 16, 16
     single, half = jnp.float32, jnp.bfloat16
     vmem, dma = pltpu.VMEM, pltpu.SemaphoreType.DMA
     held_map = vmem((width, 2 * width), half)
@@ -481,7 +552,7 @@
     return pl.pallas_call(
         functools.partial(kernel, planes),
         out_shape=jax.ShapeDtypeStruct(sources.shape, single),
-        in_specs=[any_space, any_space, any_space, in_vmem],
+        in_specs=[any_space, any_space, any_space, pl.BlockSpec(memory_space=pltpu.SMEM)],
         out_specs=in_vmem,
         scratch_shapes=[
             vmem((ROWS, 2, width, block), single),
@@ -501,15 +572,15 @@
             map_buffer,
             rows_buffer,
             rows_buffer,
-            vmem((ROWS, 2, block, width), single),
+            vmem((ROWS, block, 2 * width), single),
             held_map,
             held_map,
             rows_buffer,
             rows_buffer,
             rows_buffer,
             dma((3,)),
-            dma((3, 6)),
-            dma((3, 6)),
+            dma((2, 6)),
+            dma((2, 6)),
             dma((ROWS + 1,)),
             dma((ROWS + 1,)),
             dma((map_chunks,)),
@@ -520,11 +591,15 @@
             dma((end_chunks,)),
             dma((end_chunks,)),
             dma((end_chunks,)),
+            dma((end_chunks,)),
+            dma((3, map_chunks)),
+            dma((3, map_chunks)),
+            pltpu.SemaphoreType.REGULAR,
         ],
         compiler_params=pltpu.CompilerParams(
-            collective_id=0, has_side_effects=True, vmem_limit_bytes=60 * 2**20
+            collective_id=0, has_side_effects=True, vmem_limit_bytes=40 * 2**20
         ),
-    )(inverses, couplings, sources, active)
+    )(inverses, couplings, sources, counts)
 
 
 def solution(mesh):

time: 124 us -> 112 us (0.903)
  the two profiles are of different devices: /device:TPU:230 before, /device:TPU:228 now
where the time goes in v1:
time: 112 us; the launch traced here: 111 us
  Pallas kernels  106 us (95%)
  local copies, waits for them, and re-layouts  4.27 us (4%)
    pallas_call x1, Pallas kernels, local(): pl.pallas_call(functools.partial(kernel, planes), out_shape=jax.ShapeDtyp...  106 us
    unnamed x7, local copies, waits for them, and re-layouts  4.27 us

profile of v1, /device:TPU:228, one launch (start us, length us, event | category | flops | bytes accessed | tf_op | source)
XLA Modules:
  0.0 111.4 jit_solution(1281610835761757871)
XLA Ops:
  0.7 0.0 copy-start
  0.7 1.2 %copy-done = f32[1,2,512,256]{3,2,1,0:T(8,128)S(1)} copy-done((f32[1,2,512,256]{3,2,1,0:T(8,128)S(1)}, f32[1,2,512,256]{3,2,1,0:T(8,128)}, u32[]{:S(2)}) %copy-start) | copy-done | bytes 1048600
  1.9 0.0 copy-start.1
  1.9 1.0 copy-done.1
  2.9 0.0 copy-start.2
  2.9 1.0 copy-done.2
  4.0 106.5 %shard_map.46 = f32[1,2,512,256]{3,2,1,0:T(8,128)S(1)} custom-call(f32[1,2,512,128]{3,2,1,0:T(8,128)S(1)} %copy-done.1, f32[1,2,512,128]{3,2,1,0:T(8,128)S(1)} %copy-done.2, f32[1,2,512,256]{3,2,1,0:T(8,128)S(1)} %copy-done, s32[1]{0:T(128)S(6)} %copy.6.count_ref), custom_call_target="tpu_custom_call" | custom-call | tf_op jit(solution)/shard_map/pallas_call | solution.py:552
  110.4 1.0 copy.7
Async XLA Ops:
  0.7 1.2 %copy-start = (f32[1,2,512,256]{3,2,1,0:T(8,128)S(1)}, f32[1,2,512,256]{3,2,1,0:T(8,128)}, u32[]{:S(2)}) copy-start(f32[1,2,512,256]{3,2,1,0:T(8,128)} %source_ref.1) | copy-start | bytes 3145732
  1.9 1.0 copy-start.1
  2.9 1.0 copy-start.2

commit v2 on v1

--- a/solution.py
+++ b/solution.py
@@ -290,6 +290,31 @@
         whole_copy(0 if index < maps // 2 else 1, index).wait_recv()
         whole_copy(2, index).start()
 
+    ends = off_recv.shape[0]
+    early = ends // 2
+
+    def first_copy(index):
+        rows = rows_of(off_step, index)
+        return remote(
+            off_out.at[rows], z_in.at[rows], out_send.at[index], z_recv.at[index], at(1, 3, 1)
+        )
+
+    def offsets(index, count):
+        rows = pl.ds(pl.multiple_of(index * off_step, off_step), count * off_step)
+        for extra in range(count):
+            off_copy(index + extra).wait_recv()
+        value = product(*chunk(off_in, rows), pair_high, pair_low)
+        put(off_out, rows, plus(value, chunk(offset, rows)))
+        for extra in range(count):
+
+            @pl.when(x < 3)
+            def _():
+                off_copy(index + extra).start()
+
+            @pl.when((x == 3) & (z == 0))
+            def _():
+                first_copy(index + extra).start()
+
     @pl.when(core == 1)
     def _():
         def compose(which):
@@ -350,20 +375,12 @@
             lax.fori_loop(0, map_recv.shape[0], map_sweep, 0)
 
             def off_sweep(index, carry):
-                rows = rows_of(off_step, index)
-                off_copy(index).wait_recv()
-                value = product(*chunk(off_in, rows), pair_high, pair_low)
-                put(off_out, rows, plus(value, chunk(offset, rows)))
-
-                @pl.when(x < 3)
-                def _():
-                    off_copy(index).start()
-
+                offsets(index, 1)
                 return carry
 
             done = 0
             for index in range(maps):
-                until = max(0, 2 * index - maps // 2)
+                until = max(0, index - maps // 2)
                 if until > done:
                     lax.fori_loop(done, until, off_sweep, 0)
                     done = until
@@ -372,7 +389,11 @@
                 def _():
                     forward(index)
 
-            lax.fori_loop(done, off_recv.shape[0], off_sweep, 0)
+            lax.fori_loop(done, early, off_sweep, 0)
+
+            @pl.when((x < 3) | (z == 0))
+            def _():
+                lax.fori_loop(early, ends, off_sweep, 0)
 
         @pl.when(x < 3)
         def _():
@@ -407,8 +428,6 @@
             for index in range(maps):
                 whole_copy(kind, index).wait_send()
 
-    ends = z_recv.shape[0]
-
     def z_copy(index):
         rows = rows_of(end_step, index)
         return remote(
@@ -451,8 +470,6 @@
         def _():
             z_in[...] = jnp.zeros_like(z_in)
             state[...] = off_out[...]
-            for index in range(ends):
-                z_copy(index).start()
             for index in range(ends):
                 enter_copy(index).start()
                 enter_back_copy(index).start()
@@ -473,7 +490,13 @@
 
                 return carry
 
-            lax.fori_loop(0, ends, z_sweep, 0)
+            def both_sweep(index, carry):
+                offsets(early + 2 * index, 2)
+                z_sweep(2 * index, carry)
+                return z_sweep(2 * index + 1, carry)
+
+            lax.fori_loop(0, (ends - early) // 2, both_sweep, 0)
+            lax.fori_loop(ends - early, ends, z_sweep, 0)
 
         @pl.when(z < planes - 1)
         def _():
@@ -541,7 +564,7 @@
 def local(planes, inverses, couplings, sources, counts):
     width, block = inverses.shape[2], inverses.shape[3]
     columns = sources.shape[3]
-    map_chunks, off_chunks, end_chunks = 4, 16, 16
+    map_chunks, end_chunks = 8, 16
     single, half = jnp.float32, jnp.bfloat16
     vmem, dma = pltpu.VMEM, pltpu.SemaphoreType.DMA
     held_map = vmem((width, 2 * width), half)
@@ -585,8 +608,8 @@
             dma((ROWS + 1,)),
             dma((map_chunks,)),
             dma((map_chunks,)),
-            dma((off_chunks,)),
-            dma((off_chunks,)),
+            dma((end_chunks,)),
+            dma((end_chunks,)),
             dma((end_chunks,)),
             dma((end_chunks,)),
             dma((end_chunks,)),

time: 112 us -> 105 us (0.938)
  Pallas kernels: 106 us -> 99.8 us
    pallas_call x1, Pallas kernels: 106 us -> 99.8 us  [local(): pl.pallas_call(functools.partial(kernel, planes), out_shape=jax.ShapeDtyp...]
where the time goes in v2:
time: 105 us
  Pallas kernels  99.8 us (95%)
  local copies, waits for them, and re-layouts  4.27 us (4%)
    pallas_call x1, Pallas kernels, local(): pl.pallas_call(functools.partial(kernel, planes), out_shape=jax.ShapeDtyp...  99.8 us
    unnamed x7, local copies, waits for them, and re-layouts  4.27 us

profile of v2, /device:TPU:228, one launch (start us, length us, event | category | flops | bytes accessed | tf_op | source)
XLA Modules:
  0.0 104.7 jit_solution(16737122029118323926)
XLA Ops:
  0.7 0.0 copy-start
  0.7 1.2 %copy-done = f32[1,2,512,256]{3,2,1,0:T(8,128)S(1)} copy-done((f32[1,2,512,256]{3,2,1,0:T(8,128)S(1)}, f32[1,2,512,256]{3,2,1,0:T(8,128)}, u32[]{:S(2)}) %copy-start) | copy-done | bytes 1048600
  1.9 0.0 copy-start.1
  1.9 1.0 copy-done.1
  2.9 0.0 copy-start.2
  2.9 1.0 copy-done.2
  4.0 99.8 %shard_map.46 = f32[1,2,512,256]{3,2,1,0:T(8,128)S(1)} custom-call(f32[1,2,512,128]{3,2,1,0:T(8,128)S(1)} %copy-done.1, f32[1,2,512,128]{3,2,1,0:T(8,128)S(1)} %copy-done.2, f32[1,2,512,256]{3,2,1,0:T(8,128)S(1)} %copy-done, s32[1]{0:T(128)S(6)} %copy.6.count_ref), custom_call_target="tpu_custom_call" | custom-call | tf_op jit(solution)/shard_map/pallas_call | solution.py:575
  103.8 1.0 copy.7
Async XLA Ops:
  0.7 1.2 %copy-start = (f32[1,2,512,256]{3,2,1,0:T(8,128)S(1)}, f32[1,2,512,256]{3,2,1,0:T(8,128)}, u32[]{:S(2)}) copy-start(f32[1,2,512,256]{3,2,1,0:T(8,128)} %source_ref.1) | copy-start | bytes 3145732
  1.9 1.0 copy-start.1
  2.9 1.0 copy-start.2

commit v3 on v2

--- a/solution.py
+++ b/solution.py
@@ -110,6 +110,13 @@
     x_next, x_before = (x + 1) % 4, (x + 3) % 4
     odd, last = core == 1, (core == 1) & (x == 3)
 
+    own_inv = pltpu.make_async_copy(inverse_ref.at[0], inv.at[col], local_sem.at[0])
+    own_cpl = pltpu.make_async_copy(coupling_ref.at[0], cpl.at[col], local_sem.at[1])
+    own_src = pltpu.make_async_copy(source_ref.at[0], src, local_sem.at[2])
+    own_inv.start()
+    own_cpl.start()
+    own_src.start()
+
     barrier = pltpu.get_barrier_semaphore()
 
     def greet(when, device):
@@ -140,10 +147,10 @@
             device_id_type=MESH,
         )
 
-    def ring(own, held, which):
+    def ring(held, which):
         send, recv = gather_send.at[which], gather_recv.at[which]
         first, second = held.at[:, 0], held.at[:, 1]
-        own_first, own_second = own
+        own_first, own_second = first.at[col], second.at[col]
         return [
             remote(own_first, first.at[col], send.at[0], recv.at[0], upward),
             remote(own_second, second.at[col], send.at[1], recv.at[1], downward),
@@ -153,19 +160,13 @@
             remote(second.at[up], second.at[up], send.at[5], recv.at[5], downward),
         ]
 
-    inv_ring = ring((inverse_ref.at[0, 0], inverse_ref.at[0, 1]), inv, 0)
-    cpl_ring = ring((coupling_ref.at[0, 0], coupling_ref.at[0, 1]), cpl, 1)
-    own_inv = pltpu.make_async_copy(inverse_ref.at[0], inv.at[col], local_sem.at[0])
-    own_cpl = pltpu.make_async_copy(coupling_ref.at[0], cpl.at[col], local_sem.at[1])
-    own_src = pltpu.make_async_copy(source_ref.at[0], src, local_sem.at[2])
-    own_inv.start()
-    own_cpl.start()
-    own_src.start()
-
+    inv_ring = ring(inv, 0)
+    cpl_ring = ring(cpl, 1)
     @pl.when(core == 0)
     def _():
         pl.semaphore_wait(turn_sem, 1)
 
+    own_inv.wait()
     for copy in inv_ring[:4]:
         copy.start()
 
@@ -178,12 +179,12 @@
             inv_high[rows, part * width : (part + 1) * width] = high
             inv_low[rows, part * width : (part + 1) * width] = low
 
-    own_inv.wait()
     take_inverse(col)
     inv_ring[0].wait_recv()
     inv_ring[4].start()
     inv_ring[1].wait_recv()
     inv_ring[5].start()
+    own_cpl.wait()
     for copy in cpl_ring[:4]:
         copy.start()
     inv_ring[2].wait_recv()
@@ -213,7 +214,6 @@
             even_map[which, :, width:] = imag
             even_map_copy(which).start()
 
-    own_cpl.wait()
     take_coupling(col)
     own_src.wait()
     for start in range(0, columns, block):
@@ -354,6 +354,14 @@
         for which in (down, up, across):
             compose(which)
 
+        @pl.when(x == 0)
+        def _():
+            for index in range(maps):
+                whole_copy(0, index).start()
+                whole_copy(1, index).start()
+            for index in range(maps):
+                forward(index)
+
         @pl.when(x > 0)
         def _():
             def map_sweep(index, carry):
@@ -365,10 +373,8 @@
                 def _():
                     map_copy(index).start()
 
-                @pl.when(x == 3)
-                def _():
-                    whole_copy(0, index).start()
-                    whole_copy(1, index).start()
+                whole_copy(0, index).start()
+                whole_copy(1, index).start()
 
                 return carry
 
@@ -384,10 +390,7 @@
                 if until > done:
                     lax.fori_loop(done, until, off_sweep, 0)
                     done = until
-
-                @pl.when(x == 3)
-                def _():
-                    forward(index)
+                forward(index)
 
             lax.fori_loop(done, early, off_sweep, 0)
 
@@ -397,11 +400,6 @@
 
         @pl.when(x < 3)
         def _():
-            for index in range(maps):
-                whole_copy(0, index).start()
-                whole_copy(1, index).start()
-            for index in range(maps):
-                forward(index)
             for index in range(map_recv.shape[0]):
                 map_copy(index).wait_send()
             for index in range(off_recv.shape[0]):
@@ -570,12 +568,12 @@
     held_map = vmem((width, 2 * width), half)
     rows_buffer = vmem((columns, 2 * width), single)
     map_buffer = vmem((block, 2 * width), single)
-    any_space = pl.BlockSpec(memory_space=pl.ANY)
+    in_hbm = pl.BlockSpec(memory_space=pltpu.HBM)
     in_vmem = pl.BlockSpec(memory_space=pltpu.VMEM)
     return pl.pallas_call(
         functools.partial(kernel, planes),
         out_shape=jax.ShapeDtypeStruct(sources.shape, single),
-        in_specs=[any_space, any_space, any_space, pl.BlockSpec(memory_space=pltpu.SMEM)],
+        in_specs=[in_hbm, in_hbm, in_hbm, pl.BlockSpec(memory_space=pltpu.SMEM)],
         out_specs=in_vmem,
         scratch_shapes=[
             vmem((ROWS, 2, width, block), single),
@@ -622,7 +620,7 @@
         compiler_params=pltpu.CompilerParams(
             collective_id=0, has_side_effects=True, vmem_limit_bytes=40 * 2**20
         ),
-    )(inverses, couplings, sources, counts)
+    )(*(pltpu.with_memory_space_constraint(v, pltpu.HBM) for v in (inverses, couplings, sources)), counts)
 
 
 def solution(mesh):

time: 105 us -> 102 us (0.971)
  local copies, waits for them, and re-layouts: 4.27 us -> 0.97 us
    unnamed x7 -> x1, local copies, waits for them, and re-layouts: 4.27 us -> 0.97 us
where the time goes in v3:
time: 102 us; the launch traced here: 101 us
  Pallas kernels  99.8 us (98%)
    pallas_call x1, Pallas kernels, local(): pl.pallas_call(functools.partial(kernel, planes), out_shape=jax.ShapeDtyp...  99.8 us

profile of v3, /device:TPU:228, one launch (start us, length us, event | category | flops | bytes accessed | tf_op | source)
XLA Modules:
  0.0 101.4 jit_solution(14150651112392675191)
XLA Ops:
  0.7 99.8 %shard_map.46 = f32[1,2,512,256]{3,2,1,0:T(8,128)S(1)} custom-call(f32[1,2,512,128]{3,2,1,0:T(8,128)} %inverse_ref.1, f32[1,2,512,128]{3,2,1,0:T(8,128)} %coupling_ref.1, f32[1,2,512,256]{3,2,1,0:T(8,128)} %source_ref.1, s32[1]{0:T(128)S(6)} %copy.6.count_ref), custom_call_target="tpu_custom_call" | custom-call | tf_op jit(solution)/shard_map/pallas_call | solution.py:573
  100.5 1.0 copy.7

commit v4 on v3

--- a/solution.py
+++ b/solution.py
@@ -85,6 +85,7 @@
     back_send,
     whole_send,
     whole_recv,
+    core_pass,
     turn_sem,
 ):
     width = inv_high.shape[0]
@@ -131,8 +132,6 @@
     greeted = 3
     greeted += greet(odd, at(z, x_next, 1))
     greeted += greet(odd, at(z, x_before, 1))
-    greeted += greet(odd & (x < 3), at(z, x_next, 0))
-    greeted += greet((core == 0) & (x > 0), at(z, x_before, 1))
     greeted += greet(last & (z < planes - 1), at(z + 1, 3, 1))
     greeted += greet(last & (z > 0), at(z - 1, 3, 1))
     pl.semaphore_wait(barrier, greeted)
@@ -187,6 +186,11 @@
     own_cpl.wait()
     for copy in cpl_ring[:4]:
         copy.start()
+
+    @pl.when(core == 1)
+    def _():
+        pl.semaphore_signal(turn_sem, inc=1, device_id=partner, device_id_type=MESH)
+
     inv_ring[2].wait_recv()
     take_inverse(down)
     inv_ring[3].wait_recv()
@@ -235,10 +239,6 @@
     cpl_ring[5].start()
     cpl_ring[2].wait_recv()
     cpl_ring[3].wait_recv()
-
-    @pl.when(core == 1)
-    def _():
-        pl.semaphore_signal(turn_sem, inc=1, device_id=partner, device_id_type=MESH)
 
     take_coupling(down)
     take_coupling(up)
@@ -314,6 +314,9 @@
             @pl.when((x == 3) & (z == 0))
             def _():
                 first_copy(index + extra).start()
+
+    hand_map = remote(map_in, map_in, core_send.at[ROWS + 1], core_recv.at[ROWS + 1], partner)
+    hand_off = remote(off_in, off_in, core_send.at[ROWS + 2], core_recv.at[ROWS + 2], partner)
 
     @pl.when(core == 1)
     def _():
@@ -394,9 +397,11 @@
 
             lax.fori_loop(done, early, off_sweep, 0)
 
-            @pl.when((x < 3) | (z == 0))
+            @pl.when((x < 3) | (z != 1))
             def _():
                 lax.fori_loop(early, ends, off_sweep, 0)
+                hand_map.start()
+                hand_off.start()
 
         @pl.when(x < 3)
         def _():
@@ -405,26 +410,57 @@
             for index in range(off_recv.shape[0]):
                 off_copy(index).wait_send()
 
-        def take_whole(which):
-            rows = pl.ds(pl.multiple_of(which * block, block), block)
-            high, low = split(whole[which])
-            whole_high[rows] = high
-            whole_low[rows] = low
-
-        whole[col] = map_out[...]
-        take_whole(col)
-        for index in range(maps // 2, maps):
-            whole_copy(0, index).wait_recv()
-        take_whole(down)
-        for index in range(maps // 2):
-            whole_copy(1, index).wait_recv()
-        take_whole(up)
+    @pl.when(core == 0)
+    def _():
+        @pl.when(x == 0)
+        def _():
+            map_out[...] = even_map[col]
+            off_out[...] = offset[...]
+
+        @pl.when(x > 0)
+        def _():
+            hand_map.wait_recv()
+            put(map_out, slice(None), product(*chunk(map_in, slice(None)), own_high, own_low))
+
         for index in range(maps):
-            whole_copy(2, index).wait_recv()
-        take_whole(across)
-        for kind in range(3):
-            for index in range(maps):
-                whole_copy(kind, index).wait_send()
+            whole_copy(0, index).start()
+            whole_copy(1, index).start()
+
+        @pl.when(x > 0)
+        def _():
+            hand_off.wait_recv()
+
+            def even_offsets(index, carry):
+                rows = rows_of(block, index)
+                value = product(*chunk(off_in, rows), own_high, own_low)
+                put(off_out, rows, plus(value, chunk(offset, rows)))
+                return carry
+
+            lax.fori_loop(0, columns // block, even_offsets, 0)
+
+        for index in range(maps):
+            forward(index)
+
+    def take_whole(which):
+        rows = pl.ds(pl.multiple_of(which * block, block), block)
+        high, low = split(whole[which])
+        whole_high[rows] = high
+        whole_low[rows] = low
+
+    whole[col] = map_out[...]
+    take_whole(col)
+    for index in range(maps // 2, maps):
+        whole_copy(0, index).wait_recv()
+    take_whole(down)
+    for index in range(maps // 2):
+        whole_copy(1, index).wait_recv()
+    take_whole(up)
+    for index in range(maps):
+        whole_copy(2, index).wait_recv()
+    take_whole(across)
+    for kind in range(3):
+        for index in range(maps):
+            whole_copy(kind, index).wait_send()
 
     def z_copy(index):
         rows = rows_of(end_step, index)
@@ -456,10 +492,10 @@
             x_in.at[rows], x_in.at[rows], pass_send.at[index], x_recv.at[index], partner
         )
 
-    def x_copy(index):
+    def enter_core_copy(index):
         rows = rows_of(end_step, index)
         return remote(
-            state.at[rows], x_in.at[rows], out_send.at[index], x_recv.at[index], at(z, x_next, 0)
+            z_in.at[rows], x_in.at[rows], core_pass.at[index], x_recv.at[index], partner
         )
 
     @pl.when((core == 1) & (x == 3))
@@ -471,6 +507,7 @@
             for index in range(ends):
                 enter_copy(index).start()
                 enter_back_copy(index).start()
+                enter_core_copy(index).start()
 
         @pl.when(z > 0)
         def _():
@@ -479,6 +516,7 @@
                 z_copy(index).wait_recv()
                 enter_copy(index).start()
                 enter_back_copy(index).start()
+                enter_core_copy(index).start()
                 value = product(*chunk(z_in, rows), whole_high, whole_low)
                 put(state, rows, plus(value, chunk(off_out, rows)))
 
@@ -489,11 +527,20 @@
                 return carry
 
             def both_sweep(index, carry):
-                offsets(early + 2 * index, 2)
+                @pl.when(z == 1)
+                def _():
+                    offsets(early + 2 * index, 2)
+
                 z_sweep(2 * index, carry)
                 return z_sweep(2 * index + 1, carry)
 
             lax.fori_loop(0, (ends - early) // 2, both_sweep, 0)
+
+            @pl.when(z == 1)
+            def _():
+                hand_map.start()
+                hand_off.start()
+
             lax.fori_loop(ends - early, ends, z_sweep, 0)
 
         @pl.when(z < planes - 1)
@@ -504,50 +551,45 @@
         for index in range(ends):
             enter_copy(index).wait_send()
             enter_back_copy(index).wait_send()
-
-    @pl.when((core == 1) & (x < 3))
+            enter_core_copy(index).wait_send()
+
+    @pl.when((core == 0) | (x < 3))
     def _():
         def x_sweep(index, carry):
-            rows = rows_of(end_step, index)
-            x_copy(index).wait_recv()
-
-            @pl.when(x == 2)
+            pass_copy(index).wait_recv()
+
+            @pl.when(odd & (x == 2))
             def _():
                 back_copy(index).start()
 
-            @pl.when(x == 0)
+            @pl.when(odd)
             def _():
                 pass_copy(index).start()
 
+            rows = rows_of(end_step, index)
             value = product(*chunk(x_in, rows), whole_high, whole_low)
             put(state, rows, plus(value, chunk(off_out, rows)))
-            x_copy(index).start()
             return carry
 
         lax.fori_loop(0, ends, x_sweep, 0)
-        for index in range(ends):
-            x_copy(index).wait_send()
-
-        @pl.when(x == 2)
+
+        @pl.when(odd & (x == 2))
         def _():
             for index in range(ends):
                 back_copy(index).wait_send()
 
-        @pl.when(x == 0)
+        @pl.when(odd)
         def _():
             for index in range(ends):
                 pass_copy(index).wait_send()
 
+    @pl.when(odd & (x > 0))
+    def _():
+        hand_map.wait_send()
+        hand_off.wait_send()
+
     @pl.when(core == 0)
     def _():
-        def even_sweep(index, carry):
-            rows = rows_of(end_step, index)
-            x_copy(index).wait_recv()
-            value = product(*chunk(x_in, rows), own_high, own_low)
-            put(state, rows, plus(value, chunk(offset, rows)))
-            return carry
-
-        lax.fori_loop(0, ends, even_sweep, 0)
         for which in range(ROWS):
             even_map_copy(which).wait_send()
         even_offset_copy.wait_send()
@@ -602,8 +644,8 @@
             dma((3,)),
             dma((2, 6)),
             dma((2, 6)),
-            dma((ROWS + 1,)),
-            dma((ROWS + 1,)),
+            dma((ROWS + 3,)),
+            dma((ROWS + 3,)),
             dma((map_chunks,)),
             dma((map_chunks,)),
             dma((end_chunks,)),
@@ -615,6 +657,7 @@
             dma((end_chunks,)),
             dma((3, map_chunks)),
             dma((3, map_chunks)),
+            dma((end_chunks,)),
             pltpu.SemaphoreType.REGULAR,
         ],
         compiler_params=pltpu.CompilerParams(

time: 102 us -> 100 us (0.980)
  the two profiles are of different devices: /device:TPU:228 before, /device:TPU:226 now
where the time goes in v4:
time: 100 us
  Pallas kernels  98.5 us (98%)
    pallas_call x1, Pallas kernels, local(): pl.pallas_call(functools.partial(kernel, planes), out_shape=jax.ShapeDtyp...  98.5 us

profile of v4, /device:TPU:226, one launch (start us, length us, event | category | flops | bytes accessed | tf_op | source)
XLA Modules:
  0.0 100.2 jit_solution(888809962320509791)
XLA Ops:
  0.7 98.5 %shard_map.46 = f32[1,2,512,256]{3,2,1,0:T(8,128)S(1)} custom-call(f32[1,2,512,128]{3,2,1,0:T(8,128)} %inverse_ref.1, f32[1,2,512,128]{3,2,1,0:T(8,128)} %coupling_ref.1, f32[1,2,512,256]{3,2,1,0:T(8,128)} %source_ref.1, s32[1]{0:T(128)S(6)} %copy.6.count_ref), custom_call_target="tpu_custom_call" | custom-call | tf_op jit(solution)/shard_map/pallas_call | solution.py:615
  99.2 1.0 copy.7
